TPU v7x, 32 devices: a whole 2x2x4 slice. The times are simulated.
32 devices in a mesh: samples: 4 (over y, x), features: 4 (over z), rhs: 2 (over core).
Axes of the slice: x: 2, y: 2, z: 4, core: 2. Of those that a mesh axis runs over, the one named last changes fastest.
Arguments:
- design: bfloat16 [32768, 32768], P(('samples', 'rhs'), 'features'), may hold values from -0.03125 to 0.03125
- right_side: float32 [32768, 64], P('features', 'rhs'), may hold values from -6 to 6
- factor: bfloat16 [32768, 768], P('features', 'rhs'), may hold values from -0.03125 to 0.03125
- nystrom_values: float32 [768], replicated, may hold values from 0.5 to 3
Outputs:
- solution: float32 [32768, 64], P('features', 'rhs')
- residual: float32 [32768, 64], P('features', 'rhs')
All inputs are finite; a program needn't handle non-finite values.
Results may differ from a plain program's by a relative error of at most 0.0181.
Values may be sent and summed in bfloat16 or wider, within the bound.
A program may use at most 192 MiB of HBM per device.

v0:
```python
import jax
import jax.numpy as jnp
from jax import lax
from jax.sharding import PartitionSpec as P

ITERS = 3
ridge_weight = 1.0


def inner_prod(left, right):
    return lax.dot_general(
        left,
        right,
        (((0,), (0,)), ((), ())),
        precision=lax.Precision.HIGHEST,
        preferred_element_type=jnp.float32,
    )


def split_parts(values):
    upper = values.astype(jnp.bfloat16)
    widened = lax.optimization_barrier(upper).astype(jnp.float32)
    lower = (values - widened).astype(jnp.bfloat16)
    return (upper, lower)


def factor_inner(factor_narrow, values):
    upper, lower = split_parts(values)
    dims = (((0,), (0,)), ((), ()))
    first = lax.dot_general(factor_narrow, upper, dims, preferred_element_type=jnp.float32)
    second = lax.dot_general(factor_narrow, lower, dims, preferred_element_type=jnp.float32)
    return first + second


def factor_times(factor_narrow, values):
    upper, lower = split_parts(values)
    first = jnp.dot(factor_narrow, upper, preferred_element_type=jnp.float32)
    second = jnp.dot(factor_narrow, lower, preferred_element_type=jnp.float32)
    return first + second


def shards(design, right_side, factor, nystrom_values):
    feat_rows, col_share = right_side.shape
    shrink = (1.0 + jnp.min(nystrom_values)) / (1.0 + nystrom_values) - 1.0
    columns = lax.all_gather(right_side, "rhs", axis=1, tiled=True)
    residual = columns
    basis_rows = lax.all_gather(factor, "rhs", axis=1, tiled=True)

    def totals(values):
        return lax.psum(values, "features")

    def expand(projected):
        return factor_times(basis_rows, shrink[:, None] * projected)

    projected = totals(factor_inner(basis_rows, residual))
    direction = residual + expand(projected)
    solution = jnp.zeros_like(residual)
    for iteration in range(ITERS):
        narrow = direction.astype(jnp.bfloat16)
        apply_partial_value = jnp.dot(design, narrow, preferred_element_type=jnp.float32)
        narrow_images = lax.psum(apply_partial_value, "features").astype(jnp.bfloat16)
        feature_term = lax.dot_general(
            design, narrow_images, (((0,), (0,)), ((), ())), preferred_element_type=jnp.float32
        )
        summed = lax.psum(feature_term, ("samples", "rhs"))
        applied = summed + ridge_weight * direction
        gram_block, cross_term, image_res, image_image, factor_image = totals(
            (
                inner_prod(direction, applied),
                inner_prod(direction, residual),
                inner_prod(applied, residual),
                inner_prod(applied, applied),
                factor_inner(basis_rows, applied),
            )
        )
        gram_block = 0.5 * (gram_block + gram_block.T)
        chol_lower = jnp.linalg.cholesky(gram_block)
        unit_dir = jax.scipy.linalg.solve_triangular(chol_lower, direction.T, lower=True).T
        unit_img = jax.scipy.linalg.solve_triangular(chol_lower, applied.T, lower=True).T
        step_coef = jax.scipy.linalg.solve_triangular(chol_lower, cross_term, lower=True)
        solution = solution + jnp.dot(unit_dir, step_coef, precision=lax.Precision.HIGHEST)
        residual = residual - jnp.dot(unit_img, step_coef, precision=lax.Precision.HIGHEST)
        if iteration + 1 < ITERS:
            back_step = jax.scipy.linalg.solve_triangular(
                chol_lower, step_coef, lower=True, trans=1
            )
            projected = projected - jnp.dot(
                factor_image, back_step, precision=lax.Precision.HIGHEST
            )
            scaled = residual + expand(projected)
            image_new = image_res - jnp.dot(image_image, back_step, precision=lax.Precision.HIGHEST)
            image_new = image_new + inner_prod(factor_image, shrink[:, None] * projected)
            next_coef = -jax.scipy.linalg.solve_triangular(chol_lower, image_new, lower=True)
            direction = scaled + jnp.dot(unit_dir, next_coef, precision=lax.Precision.HIGHEST)
    column_start = lax.axis_index("rhs") * col_share
    out_sol = lax.dynamic_slice_in_dim(solution, column_start, col_share, 1)
    out_res = lax.dynamic_slice_in_dim(residual, column_start, col_share, 1)
    return (out_sol, out_res)


def solution(mesh):
    placed = (P(("samples", "rhs"), "features"), P("features", "rhs"), P("features", "rhs"), P())
    return jax.shard_map(
        shards,
        mesh=mesh,
        in_specs=placed,
        out_specs=(P("features", "rhs"), P("features", "rhs")),
        check_vma=False,
    )
```

profile of v0, /device:TPU:0, one launch (start us, length us, event | category | flops | bytes accessed | tf_op | source)
XLA Modules:
  0.0 853.2 jit_solution(9998928612973178029)
XLA Ops:
  10.0 12.9 %all-gather.3.cloned.1.call-done = f32[8192,64]{0,1:T(8,128)} async-done(((f32[8192,32]{0,1:T(8,128)}), f32[8192,64]{0,1:T(8,128)}) %all-gather.3.cloned.1.call-update) | async-done | bytes 2097168 | tf_op jit(solution)/shard_map/all_gather | solution.py:45
  24.7 25.6 %all-gather.5.cloned.1.call-done = bf16[8192,768]{1,0:T(8,128)(2,1)} async-done(((bf16[8192,384]{1,0:T(8,128)(2,1)}), bf16[8192,768]{1,0:T(8,128)(2,1)}) %all-gather.5.cloned.1.call-update) | async-done | bytes 12582928 | tf_op jit(solution)/shard_map/all_gather | solution.py:47
  50.3 7.0 convolution_bitcast_fusion.6
  58.5 3.0 convolution_add_fusion.5
  61.5 36.2 %all-reduce.15.cloned.1.call-done = f32[768,64]{0,1:T(8,128)} async-done(((f32[768,64]{0,1:T(8,128)}), f32[768,64]{0,1:T(8,128)}) %all-reduce.15.cloned.1.call-update) | async-done | bytes 196624 | tf_op jit(solution)/shard_map/psum | solution.py:50
  98.7 8.5 fusion.67
  107.2 9.8 %fusion.3 = f32[8192,64]{0,1:T(8,128)} fusion(f32[8192,64]{0,1:T(8,128)S(1)} %copy-done.1, f32[64,8192]{1,0:T(8,128)S(1)} %fusion.67, bf16[8192,768]{1,0:T(8,128)(2,1)} %all-gather.5.cloned.1.call-done, bf16[768,64]{0,1:T(8,128)(2,1)S(1)} %multiply_convert_fusion, f32[768,64]{0,1:T(8,128)S(1)} %copy-done.19, f32[768]{0:T(1024)S(1)} %divide_add_fusion), kind=kOutput, calls=%fused_computation.13 | convolution fusion | flops 806551552 | bytes 19172352 | tf_op jit(solution)/shard_map/dot_general | solution.py:38
  117.1 30.4 %convolution_bitcast_fusion.5 = f32[4096,64]{0,1:T(8,128)S(1)} fusion(bf16[4096,8192]{1,0:T(8,128)(2,1)} %param.11, f32[8192,64]{0,1:T(8,128)} %fusion.3), kind=kOutput, calls=%fused_computation.18 | convolution fusion | flops 4295491584 | bytes 70254592 | tf_op jit(solution)/shard_map/dot_general | solution.py:60
  147.4 42.8 %all-reduce.30 = bf16[4096,64]{0,1:T(8,128)(2,1)} all-reduce(f32[4096,64]{0,1:T(8,128)S(1)} %convolution_bitcast_fusion.5), channel_id=1, replica_groups=mesh['samples'=4,'features'=4,'rhs'=2] {'features'}, use_global_device_ids=true, to_apply=%region_2.0 | all-reduce | flops 262144 | bytes 1572864 | tf_op jit(solution)/shard_map/psum | solution.py:61
  190.2 25.9 %convolution_bitcast_fusion.2 = f32[8192,64]{0,1:T(8,128)} fusion(bf16[4096,8192]{1,0:T(8,128)(2,1)} %param.11, bf16[4096,64]{0,1:T(8,128)(2,1)} %all-reduce.30), kind=kOutput, calls=%fused_computation.10 | convolution fusion | flops 4294967296 | bytes 69730304 | tf_op jit(solution)/shard_map/dot_general | solution.py:62
  216.2 4.0 fusion.69
  220.2 57.3 %all-reduce.17.cloned.1.call-done = f32[8192,64]{0,1:T(8,128)} async-done(((f32[8192,64]{0,1:T(8,128)}), f32[8192,64]{0,1:T(8,128)}) %all-reduce.17.cloned.1.call-update) | async-done | bytes 2097168 | tf_op jit(solution)/shard_map/psum | solution.py:65
  277.5 2.5 fusion.65
  282.4 2.4 fusion.68
  287.3 6.8 fusion.71
  294.2 7.6 fusion.22
  302.0 19.4 %all-reduce.29.cloned.1.call-done = (f32[64,64]{1,0:T(8,128)}, f32[64,64]{1,0:T(8,128)}, f32[64,64]{1,0:T(8,128)}, f32[64,64]{1,0:T(8,128)}) async-done(((f32[64,64]{1,0:T(8,128)}, f32[64,64]{1,0:T(8,128)}, f32[64,64]{1,0:T(8,128)}, f32[64,64]{1,0:T(8,128)}), (f32[64,64]{1,0:T(8,128)}, f32[64,64]{1,0:T(8,128)}, f32[64,64]{1,0:T(8,128)}, f32[64,64]{1,0:T(8,128)})) %all-reduce.29.cloned.1.call-update) | async-done | bytes 65552 | tf_op jit(solution)/shard_map/psum | solution.py:50
  323.1 5.8 cholesky.59
  330.3 4.9 custom-call.21
  335.2 4.8 fusion.16
  344.5 14.6 %all-reduce.19.cloned.1.call-done = f32[768,64]{0,1:T(8,128)} async-done(((f32[768,64]{0,1:T(8,128)}), f32[768,64]{0,1:T(8,128)}) %all-reduce.19.cloned.1.call-update) | async-done | bytes 196624 | tf_op jit(solution)/shard_map/psum | solution.py:50
  362.1 8.4 fusion.72
  370.6 8.6 %fusion.4 = f32[8192,64]{0,1:T(8,128)S(1)} fusion(f32[8192,64]{0,1:T(8,128)S(1)} %convolution_subtract_fusion.1, f32[64,8192]{1,0:T(8,128)S(1)} %fusion.72, bf16[8192,768]{1,0:T(8,128)(2,1)} %all-gather.5.cloned.1.call-done, bf16[768,64]{0,1:T(8,128)(2,1)S(1)} %get-tuple-element.20, f32[768,64]{0,1:T(8,128)S(1)} %get-tuple-element.21, ...), kind=kOutput, calls=%fused_computation.14 | convolution fusion | flops 806551552 | bytes 19172352 | tf_op jit(solution)/shard_map/dot_general | solution.py:38
  381.5 27.8 %convolution_bitcast_fusion.4 = f32[4096,64]{0,1:T(8,128)S(1)} fusion(bf16[4096,8192]{1,0:T(8,128)(2,1)} %param.11, f32[8192,64]{0,1:T(8,128)S(1)} %convolution_add_fusion.2), kind=kOutput, calls=%fused_computation.17 | convolution fusion | flops 4295491584 | bytes 70254592 | tf_op jit(solution)/shard_map/dot_general | solution.py:60
  409.4 42.1 %all-reduce.31 = bf16[4096,64]{0,1:T(8,128)(2,1)} all-reduce(f32[4096,64]{0,1:T(8,128)S(1)} %convolution_bitcast_fusion.4), channel_id=1, replica_groups=mesh['samples'=4,'features'=4,'rhs'=2] {'features'}, use_global_device_ids=true, to_apply=%region_11.0 | all-reduce | flops 262144 | bytes 1572864 | tf_op jit(solution)/shard_map/psum | solution.py:61
  451.5 25.9 %convolution_bitcast_fusion.1 = f32[8192,64]{0,1:T(8,128)} fusion(bf16[4096,8192]{1,0:T(8,128)(2,1)} %param.11, bf16[4096,64]{0,1:T(8,128)(2,1)} %all-reduce.31), kind=kOutput, calls=%fused_computation.5 | convolution fusion | flops 4294967296 | bytes 69730304 | tf_op jit(solution)/shard_map/dot_general | solution.py:62
  477.9 4.0 fusion.76
  481.9 57.4 %all-reduce.21.cloned.1.call-done = f32[8192,64]{0,1:T(8,128)} async-done(((f32[8192,64]{0,1:T(8,128)}), f32[8192,64]{0,1:T(8,128)}) %all-reduce.21.cloned.1.call-update) | async-done | bytes 2097168 | tf_op jit(solution)/shard_map/psum | solution.py:65
  539.3 2.6 fusion.64
  549.5 6.8 fusion.78
  556.4 7.6 fusion.23
  564.2 19.4 %all-reduce.27.cloned.1.call-done = (f32[64,64]{1,0:T(8,128)}, f32[64,64]{1,0:T(8,128)}, f32[64,64]{1,0:T(8,128)}, f32[64,64]{1,0:T(8,128)}) async-done(((f32[64,64]{1,0:T(8,128)}, f32[64,64]{1,0:T(8,128)}, f32[64,64]{1,0:T(8,128)}, f32[64,64]{1,0:T(8,128)}), (f32[64,64]{1,0:T(8,128)}, f32[64,64]{1,0:T(8,128)}, f32[64,64]{1,0:T(8,128)}, f32[64,64]{1,0:T(8,128)})) %all-reduce.27.cloned.1.call-update) | async-done | bytes 65552 | tf_op jit(solution)/shard_map/psum | solution.py:50
  585.3 5.8 cholesky.70
  592.5 4.9 custom-call.26
  597.4 4.8 fusion.12
  606.6 14.8 %all-reduce.23.cloned.1.call-done = f32[768,64]{0,1:T(8,128)} async-done(((f32[768,64]{0,1:T(8,128)}), f32[768,64]{0,1:T(8,128)}) %all-reduce.23.cloned.1.call-update) | async-done | bytes 196624 | tf_op jit(solution)/shard_map/psum | solution.py:50
  624.5 8.4 fusion.79
  632.9 8.6 %fusion.5 = f32[8192,64]{0,1:T(8,128)S(1)} fusion(f32[8192,64]{0,1:T(8,128)S(1)} %convolution_subtract_fusion, f32[64,8192]{1,0:T(8,128)S(1)} %fusion.79, bf16[8192,768]{1,0:T(8,128)(2,1)} %all-gather.5.cloned.1.call-done, f32[768,64]{0,1:T(8,128)S(1)} %get-tuple-element.23, bf16[768,64]{0,1:T(8,128)(2,1)S(1)} %get-tuple-element.22), kind=kOutput, calls=%fused_computation.15 | convolution fusion | flops 806502400 | bytes 19169280 | tf_op jit(solution)/shard_map/dot_general | solution.py:38
  644.0 27.1 %convolution_bitcast_fusion.3 = f32[4096,64]{0,1:T(8,128)S(1)} fusion(bf16[4096,8192]{1,0:T(8,128)(2,1)} %param.11, f32[8192,64]{0,1:T(8,128)S(1)} %convolution_add_fusion), kind=kOutput, calls=%fused_computation.16 | convolution fusion | flops 4295491584 | bytes 70254592 | tf_op jit(solution)/shard_map/dot_general | solution.py:60
  671.1 42.1 %all-reduce.32 = bf16[4096,64]{0,1:T(8,128)(2,1)} all-reduce(f32[4096,64]{0,1:T(8,128)S(1)} %convolution_bitcast_fusion.3), channel_id=1, replica_groups=mesh['samples'=4,'features'=4,'rhs'=2] {'features'}, use_global_device_ids=true, to_apply=%region_18.0 | all-reduce | flops 262144 | bytes 1572864 | tf_op jit(solution)/shard_map/psum | solution.py:61
  713.2 25.9 %convolution_bitcast_fusion = f32[8192,64]{0,1:T(8,128)} fusion(bf16[4096,8192]{1,0:T(8,128)(2,1)} %param.11, bf16[4096,64]{0,1:T(8,128)(2,1)} %all-reduce.32), kind=kOutput, calls=%fused_computation | convolution fusion | flops 4294967296 | bytes 69730304 | tf_op jit(solution)/shard_map/dot_general | solution.py:62
  739.9 5.0 fusion.70
  744.9 3.3 fusion.77
  750.0 50.6 %all-reduce.25.cloned.1.call-done = f32[8192,64]{0,1:T(8,128)} async-done(((f32[8192,64]{0,1:T(8,128)}), f32[8192,64]{0,1:T(8,128)}) %all-reduce.25.cloned.1.call-update) | async-done | bytes 2097168 | tf_op jit(solution)/shard_map/psum | solution.py:65
  800.6 3.5 fusion.19
  804.1 19.8 %all-reduce = (f32[64,64]{1,0:T(8,128)S(1)}, f32[64,64]{1,0:T(8,128)S(1)}) all-reduce(f32[64,64]{1,0:T(8,128)S(1)} %fusion.19, f32[64,64]{1,0:T(8,128)S(1)} %fusion.83), channel_id=1, replica_groups=mesh['samples'=4,'features'=4,'rhs'=2] {'features'}, use_global_device_ids=true, to_apply=%region_20.25 | all-reduce | flops 8192 | bytes 65536 | tf_op jit(solution)/shard_map/psum | solution.py:50
  824.1 5.8 cholesky.81
  831.2 4.9 custom-call.31
  (133 shorter events, 59.0 us)
Async XLA Ops:
  7.2 15.7 %all-gather.3.cloned.1.call-start = ((), (), s32[]{:S(2)}) async-start(), calls=%async_computation | async-start | bytes 3145728 | tf_op jit(solution)/shard_map/all_gather | solution.py:45
  7.9 0.8 copy-start.28
  7.9 42.4 %all-gather.5.cloned.1.call-start = ((), (), s32[]{:S(2)}) async-start(), calls=%async_computation.1 | async-start | bytes 18874368 | tf_op jit(solution)/shard_map/all_gather | solution.py:47
  8.7 89.1 %all-reduce.15.cloned.1.call-start = ((), (), s32[]{:S(2)}) async-start(), calls=%async_computation.2 | async-start | bytes 393216 | tf_op jit(solution)/shard_map/psum | solution.py:50
  22.8 27.4 %copy-start.1 = (f32[8192,64]{0,1:T(8,128)S(1)}, f32[8192,64]{0,1:T(8,128)}, u32[]{:S(2)}) copy-start(f32[8192,64]{0,1:T(8,128)} %all-gather.3.cloned.1.call-done) | copy-start | bytes 6291460
  50.3 8.2 copy-start
  61.5 216.0 %all-reduce.17.cloned.1.call-start = ((), (), s32[]{:S(2)}) async-start(), calls=%async_computation.3 | async-start | bytes 4194304 | tf_op jit(solution)/shard_map/psum | solution.py:65
  98.7 8.5 copy-start.19
  216.2 105.3 %all-reduce.29.cloned.1.call-start = ((), (), s32[]{:S(2)}) async-start(), calls=%async_computation.9 | async-start | bytes 262144 | tf_op jit(solution)/shard_map/psum | solution.py:50
  280.0 2.4 copy-start.4
  282.4 2.4 copy-start.2
  287.3 71.8 %all-reduce.19.cloned.1.call-start = ((), (), s32[]{:S(2)}) async-start(), calls=%async_computation.4 | async-start | bytes 393216 | tf_op jit(solution)/shard_map/psum | solution.py:50
  301.8 237.5 %all-reduce.21.cloned.1.call-start = ((), (), s32[]{:S(2)}) async-start(), calls=%async_computation.5 | async-start | bytes 4194304 | tf_op jit(solution)/shard_map/psum | solution.py:65
  340.0 1.9 copy-start.26
  340.0 2.2 copy-start.3
  342.2 2.1 copy-start.20
  342.2 19.4 %copy-start.24 = (f32[64,64]{1,0:T(8,128)S(1)}, f32[64,64]{1,0:T(8,128)}, u32[]{:S(2)}) copy-start(f32[64,64]{1,0:T(8,128)} %get-tuple-element.14) | copy-start | bytes 49156
  342.2 19.4 %copy-start.25 = (f32[64,64]{1,0:T(8,128)S(1)}, f32[64,64]{1,0:T(8,128)}, u32[]{:S(2)}) copy-start(f32[64,64]{1,0:T(8,128)} %get-tuple-element.15) | copy-start | bytes 49156
  344.3 26.2 %copy-start.7 = (f32[8192,64]{0,1:T(8,128)}, f32[8192,64]{0,1:T(8,128)S(1)}, u32[]{:S(2)}) copy-start(f32[8192,64]{0,1:T(8,128)S(1)} %convolution_subtract_fusion.1) | copy-start | bytes 6291460
  370.5 8.7 %copy-start.13 = (f32[64,8192]{1,0:T(8,128)S(1)}, f32[64,8192]{1,0:T(8,128)}, u32[]{:S(2)}) copy-start(f32[64,8192]{1,0:T(8,128)} %fusion.16) | copy-start | bytes 6291460
  381.5 96.4 %copy-start.5 = (f32[8192,64]{0,1:T(8,128)}, f32[8192,64]{0,1:T(8,128)S(1)}, u32[]{:S(2)}) copy-start(f32[8192,64]{0,1:T(8,128)S(1)} %convolution_add_fusion.2) | copy-start | bytes 6291460
  477.5 106.1 %all-reduce.27.cloned.1.call-start = ((), (), s32[]{:S(2)}) async-start(), calls=%async_computation.8 | async-start | bytes 262144 | tf_op jit(solution)/shard_map/psum | solution.py:50
  539.3 2.9 copy-start.8
  544.6 2.4 copy-start.6
  549.5 72.0 %all-reduce.23.cloned.1.call-start = ((), (), s32[]{:S(2)}) async-start(), calls=%async_computation.6 | async-start | bytes 393216 | tf_op jit(solution)/shard_map/psum | solution.py:50
  564.0 236.7 %all-reduce.25.cloned.1.call-start = ((), (), s32[]{:S(2)}) async-start(), calls=%async_computation.7 | async-start | bytes 4194304 | tf_op jit(solution)/shard_map/psum | solution.py:65
  602.2 1.9 copy-start.27
  602.2 2.2 copy-start.9
  604.4 19.7 %copy-start.22 = (f32[64,64]{1,0:T(8,128)S(1)}, f32[64,64]{1,0:T(8,128)}, u32[]{:S(2)}) copy-start(f32[64,64]{1,0:T(8,128)} %get-tuple-element.10) | copy-start | bytes 49156
  604.4 19.7 %copy-start.23 = (f32[64,64]{1,0:T(8,128)S(1)}, f32[64,64]{1,0:T(8,128)}, u32[]{:S(2)}) copy-start(f32[64,64]{1,0:T(8,128)} %get-tuple-element.11) | copy-start | bytes 49156
  606.5 26.5 %copy-start.10 = (f32[8192,64]{0,1:T(8,128)}, f32[8192,64]{0,1:T(8,128)S(1)}, u32[]{:S(2)}) copy-start(f32[8192,64]{0,1:T(8,128)S(1)} %convolution_subtract_fusion) | copy-start | bytes 6291460
  632.9 8.6 %copy-start.14 = (f32[64,8192]{1,0:T(8,128)S(1)}, f32[64,8192]{1,0:T(8,128)}, u32[]{:S(2)}) copy-start(f32[64,8192]{1,0:T(8,128)} %fusion.12) | copy-start | bytes 6291460
  739.1 0.8 copy-start.21
  739.9 5.0 copy-start.15
  744.9 3.3 copy-start.11
  838.3 2.0 copy-start.16
  840.4 4.1 copy-start.18
  842.4 2.0 copy-start.12
  842.4 2.2 copy-start.17
Sparse Core Ops, SparseCore 0:
  9.5 13.2 all-gather.2
  24.4 25.8 all-gather.4
  61.6 36.1 all-reduce.14
  216.3 61.1 all-reduce.16
  287.4 33.9 all-reduce.28
  324.2 34.8 all-reduce.18
  477.6 61.6 all-reduce.20
  549.6 33.9 all-reduce.26
  586.5 34.9 all-reduce.22
  739.3 61.3 all-reduce.24
where the time goes:
time: 862 us; the launch traced here: 853 us
  matrix products  328 us (38%)
  waiting for transfers between devices  310 us (36%)
  blocking collectives  147 us (17%)
  other arithmetic  47.9 us (6%)
  between operations  15.6 us (2%)
    psum x3, waiting for transfers between devices, shards(): summed = lax.psum(feature_term, ('samples', 'rhs'))  165 us
    psum x3, blocking collectives, shards(): lax.psum(apply_partial_value, 'features').astype(jnp.bfloat16)  127 us
    psum x5, waiting for transfers between devices, totals(): return lax.psum(values, 'features')  105 us
    dot_general x3, matrix products, shards(): jnp.dot(design, narrow, preferred_element_type=jnp.float32)  85.3 us
    dot_general x3, matrix products, shards(): lax.dot_general(design, narrow_images, (((0,), (0,)), ((), ())), preferre...  77.8 us
    dot_general x12, matrix products, inner_prod(): lax.dot_general(left, right, (((0,), (0,)), ((), ())), precision=lax.Prec...  30.3 us
    dot_general x3, matrix products, factor_times(): second = jnp.dot(factor_narrow, lower, preferred_element_type=jnp.float32)  27.1 us
    all_gather x1, waiting for transfers between devices, shards(): basis_rows = lax.all_gather(factor, 'rhs', axis=1, tiled=True)  25.6 us
  transfers between devices with their start and end apart: 10, of which 10 were waited for; matrix products, arithmetic and copies ran while one was open for 11% of the time, Pallas kernels for 0%

commit v1 on v0

--- a/solution.py
+++ b/solution.py
@@ -62,7 +62,7 @@
         feature_term = lax.dot_general(
             design, narrow_images, (((0,), (0,)), ((), ())), preferred_element_type=jnp.float32
         )
-        summed = lax.psum(feature_term, ("samples", "rhs"))
+        summed = jnp.sum(lax.all_gather(feature_term, ("samples", "rhs")), axis=0)
         applied = summed + ridge_weight * direction
         gram_block, cross_term, image_res, image_image, factor_image = totals(
             (

time: 862 us -> 1020 us (1.18)
  waiting for transfers between devices: 310 us -> 397 us
  local copies, waits for them, and re-layouts: 4.31 us -> 52.8 us
  blocking collectives: 147 us -> 159 us
  other arithmetic: 47.9 us -> 58.9 us
    all_gather x0 -> x3, waiting for transfers between devices: none -> 249 us  [shards(): summed = jnp.sum(lax.all_gather(feature_term, ('samples', 'rhs')), axis=0)]
    psum x3 -> x0, waiting for transfers between devices: 165 us -> none  [shards(): summed = lax.psum(feature_term, ('samples', 'rhs'))]
    unnamed x58 -> x65, local copies, waits for them, and re-layouts: 2.36 us -> 50.8 us
    reduce_sum x0 -> x3, other arithmetic: none -> 15.6 us  [shards(): summed = jnp.sum(lax.all_gather(feature_term, ('samples', 'rhs')), axis=0)]
    psum x3, blocking collectives: 127 us -> 139 us  [shards(): lax.psum(apply_partial_value, 'features').astype(jnp.bfloat16)]
  transfers between devices with their start and end apart: 10 -> 10, of which waited for: 10 -> 10; matrix products, arithmetic and copies ran while one was open for 11% -> 9% of each run, Pallas kernels for 0% -> 0%
where the time goes in v1:
time: 1020 us; the launch traced here: 1010 us
  waiting for transfers between devices  397 us (39%)
  matrix products  324 us (32%)
  blocking collectives  159 us (16%)
  other arithmetic  58.9 us (6%)
  local copies, waits for them, and re-layouts  52.8 us (5%)
  between operations  16 us (2%)
    all_gather x3, waiting for transfers between devices, shards(): summed = jnp.sum(lax.all_gather(feature_term, ('samples', 'rhs')), axis=0)  249 us
    psum x3, blocking collectives, shards(): lax.psum(apply_partial_value, 'features').astype(jnp.bfloat16)  139 us
    psum x5, waiting for transfers between devices, totals(): return lax.psum(values, 'features')  107 us
    dot_general x3, matrix products, shards(): jnp.dot(design, narrow, preferred_element_type=jnp.float32)  85.3 us
    dot_general x3, matrix products, shards(): lax.dot_general(design, narrow_images, (((0,), (0,)), ((), ())), preferre...  77.8 us
    unnamed x65, local copies, waits for them, and re-layouts  50.8 us
    dot_general x12, matrix products, inner_prod(): lax.dot_general(left, right, (((0,), (0,)), ((), ())), precision=lax.Prec...  28.7 us
    dot_general x3, matrix products, factor_times(): second = jnp.dot(factor_narrow, lower, preferred_element_type=jnp.float32)  27.1 us
  transfers between devices with their start and end apart: 10, of which 10 were waited for; matrix products, arithmetic and copies ran while one was open for 9% of the time, Pallas kernels for 0%

profile of v1, /device:TPU:0, one launch (start us, length us, event | category | flops | bytes accessed | tf_op | source)
XLA Modules:
  0.0 1009.1 jit_solution(7697882092860864411)
XLA Ops:
  10.0 12.9 %all-gather.9.cloned.1.call-done = f32[8192,64]{0,1:T(8,128)} async-done(((f32[8192,32]{0,1:T(8,128)}), f32[8192,64]{0,1:T(8,128)}) %all-gather.9.cloned.1.call-update) | async-done | bytes 2097168 | tf_op jit(solution)/shard_map/all_gather | solution.py:45
  24.7 25.6 %all-gather.11.cloned.1.call-done = bf16[8192,768]{1,0:T(8,128)(2,1)} async-done(((bf16[8192,384]{1,0:T(8,128)(2,1)}), bf16[8192,768]{1,0:T(8,128)(2,1)}) %all-gather.11.cloned.1.call-update) | async-done | bytes 12582928 | tf_op jit(solution)/shard_map/all_gather | solution.py:47
  50.3 7.0 convolution_bitcast_fusion.6
  61.5 36.3 %all-reduce.12.cloned.1.call-done = f32[768,64]{0,1:T(8,128)} async-done(((f32[768,64]{0,1:T(8,128)}), f32[768,64]{0,1:T(8,128)}) %all-reduce.12.cloned.1.call-update) | async-done | bytes 196624 | tf_op jit(solution)/shard_map/psum | solution.py:50
  98.7 8.5 fusion.67
  107.2 9.8 fusion.3
  117.1 30.4 %convolution_bitcast_fusion.5 = f32[4096,64]{0,1:T(8,128)S(1)} fusion(bf16[4096,8192]{1,0:T(8,128)(2,1)} %param.11, f32[8192,64]{0,1:T(8,128)} %fusion.3), kind=kOutput, calls=%fused_computation.21 | convolution fusion | flops 4295491584 | bytes 70254592 | tf_op jit(solution)/shard_map/dot_general | solution.py:60
  147.5 55.1 %all-reduce.21 = bf16[4096,64]{0,1:T(8,128)(2,1)} all-reduce(f32[4096,64]{0,1:T(8,128)S(1)} %convolution_bitcast_fusion.5), channel_id=1, replica_groups=mesh['samples'=4,'features'=4,'rhs'=2] {'features'}, use_global_device_ids=true, to_apply=%region_2.0 | all-reduce | flops 262144 | bytes 1572864 | tf_op jit(solution)/shard_map/psum | solution.py:61
  202.6 25.9 %convolution_bitcast_fusion.2 = f32[8192,64]{0,1:T(8,128)} fusion(bf16[4096,8192]{1,0:T(8,128)(2,1)} %param.11, bf16[4096,64]{0,1:T(8,128)(2,1)} %all-reduce.21), kind=kOutput, calls=%fused_computation.13 | convolution fusion | flops 4294967296 | bytes 69730304 | tf_op jit(solution)/shard_map/dot_general | solution.py:62
  228.6 4.0 fusion.69
  232.6 85.4 %all-gather.13.cloned.1.call-done = f32[65536,64]{0,1:T(8,128)} async-done(((f32[8192,64]{0,1:T(8,128)}), f32[65536,64]{0,1:T(8,128)}) %all-gather.13.cloned.1.call-update) | async-done | bytes 16777232 | tf_op jit(solution)/shard_map/all_gather | solution.py:65
  317.9 15.2 %copy.12 = f32[8,8,8,8192]{3,2,1,0:T(8,128)S(1)} copy(f32[8,8,8,8192]{3,1,2,0:T(8,128)} %bitcast.223) | data formatting | bytes 33554432
  333.2 5.2 bitcast_reduce_fusion.2
  346.0 6.8 fusion.71
  352.8 7.6 fusion.22
  360.9 20.1 %all-reduce.20.cloned.1.call-done = (f32[64,64]{1,0:T(8,128)}, f32[64,64]{1,0:T(8,128)}, f32[64,64]{1,0:T(8,128)}, f32[64,64]{1,0:T(8,128)}) async-done(((f32[64,64]{1,0:T(8,128)}, f32[64,64]{1,0:T(8,128)}, f32[64,64]{1,0:T(8,128)}, f32[64,64]{1,0:T(8,128)}), (f32[64,64]{1,0:T(8,128)}, f32[64,64]{1,0:T(8,128)}, f32[64,64]{1,0:T(8,128)}, f32[64,64]{1,0:T(8,128)})) %all-reduce.20.cloned.1.call-update) | async-done | bytes 65552 | tf_op jit(solution)/shard_map/psum | solution.py:50
  382.7 5.8 cholesky.59
  389.9 4.9 custom-call.21
  402.5 16.1 %all-reduce.14.cloned.1.call-done = f32[768,64]{0,1:T(8,128)} async-done(((f32[768,64]{0,1:T(8,128)}), f32[768,64]{0,1:T(8,128)}) %all-reduce.14.cloned.1.call-update) | async-done | bytes 196624 | tf_op jit(solution)/shard_map/psum | solution.py:50
  421.6 8.4 fusion.72
  430.1 8.6 fusion.4
  441.0 27.8 %convolution_bitcast_fusion.4 = f32[4096,64]{0,1:T(8,128)S(1)} fusion(bf16[4096,8192]{1,0:T(8,128)(2,1)} %param.11, f32[8192,64]{0,1:T(8,128)S(1)} %convolution_add_fusion.2), kind=kOutput, calls=%fused_computation.20 | convolution fusion | flops 4295491584 | bytes 70254592 | tf_op jit(solution)/shard_map/dot_general | solution.py:60
  468.9 42.1 %all-reduce.22 = bf16[4096,64]{0,1:T(8,128)(2,1)} all-reduce(f32[4096,64]{0,1:T(8,128)S(1)} %convolution_bitcast_fusion.4), channel_id=1, replica_groups=mesh['samples'=4,'features'=4,'rhs'=2] {'features'}, use_global_device_ids=true, to_apply=%region_11.0 | all-reduce | flops 262144 | bytes 1572864 | tf_op jit(solution)/shard_map/psum | solution.py:61
  511.0 25.9 %convolution_bitcast_fusion.1 = f32[8192,64]{0,1:T(8,128)} fusion(bf16[4096,8192]{1,0:T(8,128)(2,1)} %param.11, bf16[4096,64]{0,1:T(8,128)(2,1)} %all-reduce.22), kind=kOutput, calls=%fused_computation.8 | convolution fusion | flops 4294967296 | bytes 69730304 | tf_op jit(solution)/shard_map/dot_general | solution.py:62
  537.0 4.0 fusion.76
  541.0 85.4 %all-gather.15.cloned.1.call-done = f32[65536,64]{0,1:T(8,128)} async-done(((f32[8192,64]{0,1:T(8,128)}), f32[65536,64]{0,1:T(8,128)}) %all-gather.15.cloned.1.call-update) | async-done | bytes 16777232 | tf_op jit(solution)/shard_map/all_gather | solution.py:65
  626.4 15.4 %copy.13 = f32[8,8,8,8192]{3,2,1,0:T(8,128)S(1)} copy(f32[8,8,8,8192]{3,1,2,0:T(8,128)} %bitcast.224) | data formatting | bytes 33554432
  641.8 5.2 bitcast_reduce_fusion.1
  655.9 6.8 fusion.78
  662.8 7.6 fusion.23
  670.9 20.0 %all-reduce.18.cloned.1.call-done = (f32[64,64]{1,0:T(8,128)}, f32[64,64]{1,0:T(8,128)}, f32[64,64]{1,0:T(8,128)}, f32[64,64]{1,0:T(8,128)}) async-done(((f32[64,64]{1,0:T(8,128)}, f32[64,64]{1,0:T(8,128)}, f32[64,64]{1,0:T(8,128)}, f32[64,64]{1,0:T(8,128)}), (f32[64,64]{1,0:T(8,128)}, f32[64,64]{1,0:T(8,128)}, f32[64,64]{1,0:T(8,128)}, f32[64,64]{1,0:T(8,128)})) %all-reduce.18.cloned.1.call-update) | async-done | bytes 65552 | tf_op jit(solution)/shard_map/psum | solution.py:50
  692.7 5.8 cholesky.70
  699.8 4.9 custom-call.26
  704.7 4.9 fusion.12
  714.1 14.8 %all-reduce.16.cloned.1.call-done = f32[768,64]{0,1:T(8,128)} async-done(((f32[768,64]{0,1:T(8,128)}), f32[768,64]{0,1:T(8,128)}) %all-reduce.16.cloned.1.call-update) | async-done | bytes 196624 | tf_op jit(solution)/shard_map/psum | solution.py:50
  731.8 8.4 fusion.79
  740.3 8.6 fusion.5
  751.1 27.1 %convolution_bitcast_fusion.3 = f32[4096,64]{0,1:T(8,128)S(1)} fusion(bf16[4096,8192]{1,0:T(8,128)(2,1)} %param.11, f32[8192,64]{0,1:T(8,128)S(1)} %convolution_add_fusion), kind=kOutput, calls=%fused_computation.19 | convolution fusion | flops 4295491584 | bytes 70254592 | tf_op jit(solution)/shard_map/dot_general | solution.py:60
  778.2 42.1 %all-reduce.23 = bf16[4096,64]{0,1:T(8,128)(2,1)} all-reduce(f32[4096,64]{0,1:T(8,128)S(1)} %convolution_bitcast_fusion.3), channel_id=1, replica_groups=mesh['samples'=4,'features'=4,'rhs'=2] {'features'}, use_global_device_ids=true, to_apply=%region_18.0 | all-reduce | flops 262144 | bytes 1572864 | tf_op jit(solution)/shard_map/psum | solution.py:61
  820.3 26.0 %convolution_bitcast_fusion = f32[8192,64]{0,1:T(8,128)} fusion(bf16[4096,8192]{1,0:T(8,128)(2,1)} %param.11, bf16[4096,64]{0,1:T(8,128)(2,1)} %all-reduce.23), kind=kOutput, calls=%fused_computation.3 | convolution fusion | flops 4294967296 | bytes 69730304 | tf_op jit(solution)/shard_map/dot_general | solution.py:62
  847.1 5.0 fusion.70
  852.0 3.3 fusion.77
  857.2 78.6 %all-gather.17.cloned.1.call-done = f32[65536,64]{0,1:T(8,128)} async-done(((f32[8192,64]{0,1:T(8,128)}), f32[65536,64]{0,1:T(8,128)}) %all-gather.17.cloned.1.call-update) | async-done | bytes 16777232 | tf_op jit(solution)/shard_map/all_gather | solution.py:65
  935.7 15.4 %copy.14 = f32[8,8,8,8192]{3,2,1,0:T(8,128)S(1)} copy(f32[8,8,8,8192]{3,1,2,0:T(8,128)} %bitcast.222) | data formatting | bytes 33554432
  951.1 5.2 bitcast_reduce_fusion
  959.6 19.9 %all-reduce = (f32[64,64]{1,0:T(8,128)S(1)}, f32[64,64]{1,0:T(8,128)S(1)}) all-reduce(f32[64,64]{1,0:T(8,128)S(1)} %fusion.19, f32[64,64]{1,0:T(8,128)S(1)} %fusion.83), channel_id=1, replica_groups=mesh['samples'=4,'features'=4,'rhs'=2] {'features'}, use_global_device_ids=true, to_apply=%region_20.25 | all-reduce | flops 8192 | bytes 65536 | tf_op jit(solution)/shard_map/psum | solution.py:50
  979.7 5.8 cholesky.81
  986.9 4.9 custom-call.31
  (143 shorter events, 72.2 us)
Async XLA Ops:
  7.2 15.7 %all-gather.9.cloned.1.call-start = ((), (), s32[]{:S(2)}) async-start(), calls=%async_computation | async-start | bytes 3145728 | tf_op jit(solution)/shard_map/all_gather | solution.py:45
  7.9 0.8 copy-start.30
  7.9 42.4 %all-gather.11.cloned.1.call-start = ((), (), s32[]{:S(2)}) async-start(), calls=%async_computation.1 | async-start | bytes 18874368 | tf_op jit(solution)/shard_map/all_gather | solution.py:47
  8.7 89.1 %all-reduce.12.cloned.1.call-start = ((), (), s32[]{:S(2)}) async-start(), calls=%async_computation.2 | async-start | bytes 393216 | tf_op jit(solution)/shard_map/psum | solution.py:50
  22.8 27.4 %copy-start.1 = (f32[8192,64]{0,1:T(8,128)S(1)}, f32[8192,64]{0,1:T(8,128)}, u32[]{:S(2)}) copy-start(f32[8192,64]{0,1:T(8,128)} %all-gather.9.cloned.1.call-done) | copy-start | bytes 6291460
  50.3 8.2 copy-start
  61.5 256.5 %all-gather.13.cloned.1.call-start = ((), (), s32[]{:S(2)}) async-start(), calls=%async_computation.5 | async-start | bytes 18874368 | tf_op jit(solution)/shard_map/all_gather | solution.py:65
  98.7 8.5 copy-start.21
  228.5 152.5 %all-reduce.20.cloned.1.call-start = ((), (), s32[]{:S(2)}) async-start(), calls=%async_computation.9 | async-start | bytes 262144 | tf_op jit(solution)/shard_map/psum | solution.py:50
  333.2 5.2 copy-start.4
  341.1 2.4 copy-start.2
  345.9 72.7 %all-reduce.14.cloned.1.call-start = ((), (), s32[]{:S(2)}) async-start(), calls=%async_computation.3 | async-start | bytes 393216 | tf_op jit(solution)/shard_map/psum | solution.py:50
  360.4 265.9 %all-gather.15.cloned.1.call-start = ((), (), s32[]{:S(2)}) async-start(), calls=%async_computation.6 | async-start | bytes 18874368 | tf_op jit(solution)/shard_map/all_gather | solution.py:65
  394.8 1.9 copy-start.5
  396.7 3.3 copy-start.28
  396.7 3.5 copy-start.3
  400.2 2.1 copy-start.22
  400.2 21.0 %copy-start.26 = (f32[64,64]{1,0:T(8,128)S(1)}, f32[64,64]{1,0:T(8,128)}, u32[]{:S(2)}) copy-start(f32[64,64]{1,0:T(8,128)} %get-tuple-element.14) | copy-start | bytes 49156
  400.2 21.0 %copy-start.27 = (f32[64,64]{1,0:T(8,128)S(1)}, f32[64,64]{1,0:T(8,128)}, u32[]{:S(2)}) copy-start(f32[64,64]{1,0:T(8,128)} %get-tuple-element.15) | copy-start | bytes 49156
  402.3 27.8 %copy-start.8 = (f32[8192,64]{0,1:T(8,128)}, f32[8192,64]{0,1:T(8,128)S(1)}, u32[]{:S(2)}) copy-start(f32[8192,64]{0,1:T(8,128)S(1)} %convolution_subtract_fusion.1) | copy-start | bytes 6291460
  430.1 8.7 copy-start.16
  441.0 96.0 %copy-start.6 = (f32[8192,64]{0,1:T(8,128)}, f32[8192,64]{0,1:T(8,128)S(1)}, u32[]{:S(2)}) copy-start(f32[8192,64]{0,1:T(8,128)S(1)} %convolution_add_fusion.2) | copy-start | bytes 6291460
  536.9 154.0 %all-reduce.18.cloned.1.call-start = ((), (), s32[]{:S(2)}) async-start(), calls=%async_computation.8 | async-start | bytes 262144 | tf_op jit(solution)/shard_map/psum | solution.py:50
  641.8 5.2 copy-start.7
  647.0 1.6 copy-start.9
  655.9 73.0 %all-reduce.16.cloned.1.call-start = ((), (), s32[]{:S(2)}) async-start(), calls=%async_computation.4 | async-start | bytes 393216 | tf_op jit(solution)/shard_map/psum | solution.py:50
  670.4 265.4 %all-gather.17.cloned.1.call-start = ((), (), s32[]{:S(2)}) async-start(), calls=%async_computation.7 | async-start | bytes 18874368 | tf_op jit(solution)/shard_map/all_gather | solution.py:65
  709.6 1.9 copy-start.29
  709.6 2.2 copy-start.10
  711.8 19.6 %copy-start.24 = (f32[64,64]{1,0:T(8,128)S(1)}, f32[64,64]{1,0:T(8,128)}, u32[]{:S(2)}) copy-start(f32[64,64]{1,0:T(8,128)} %get-tuple-element.10) | copy-start | bytes 49156
  711.8 19.6 %copy-start.25 = (f32[64,64]{1,0:T(8,128)S(1)}, f32[64,64]{1,0:T(8,128)}, u32[]{:S(2)}) copy-start(f32[64,64]{1,0:T(8,128)} %get-tuple-element.11) | copy-start | bytes 49156
  713.9 26.4 %copy-start.11 = (f32[8192,64]{0,1:T(8,128)}, f32[8192,64]{0,1:T(8,128)S(1)}, u32[]{:S(2)}) copy-start(f32[8192,64]{0,1:T(8,128)S(1)} %convolution_subtract_fusion) | copy-start | bytes 6291460
  740.3 8.6 copy-start.17
  846.3 0.8 copy-start.23
  847.1 5.0 copy-start.18
  852.0 3.3 copy-start.12
  956.4 1.3 copy-start.14
  991.8 1.9 copy-start.15
  996.0 4.1 copy-start.20
  998.0 2.1 copy-start.13
  998.0 2.2 copy-start.19
Sparse Core Ops, SparseCore 0:
  9.5 13.2 all-gather.8
  24.4 25.8 all-gather.10
  61.6 36.1 all-reduce.11
  228.6 89.2 all-gather.12
  346.1 34.8 all-reduce.19
  383.7 34.8 all-reduce.13
  537.1 89.2 all-gather.14
  656.0 34.9 all-reduce.17
  693.9 34.9 all-reduce.15
  846.4 89.2 all-gather.16
